TPU v7x, 32 devices: a whole 2x2x4 slice. The times are simulated.
32 devices in a mesh: groups: 2 (over y), ep: 4 (over z), sub: 4 (over x, core).
Axes of the slice: x: 2, y: 2, z: 4, core: 2. Of those that a mesh axis runs over, the one named last changes fastest.
Arguments:
- tokens: bfloat16 [512, 7168], P(('groups', 'ep'), 'sub'), parts along dimension 0, may hold values from -6 to 6
- expert_ids: int32 [512, 2], P(('groups', 'ep')), parts along dimension 0, may hold values from 0 to 3, all different within a row; in each aligned block of 64 rows (0 to 63, 64 to 127, ...) at most 48 rows name the same one
- route_weights: float32 [512, 2], P(('groups', 'ep')), parts along dimension 0, may hold values from 0.05 to 0.6
- gate_weight: bfloat16 [4, 7168, 1024], P('ep', 'sub'), may hold values from -0.0625 to 0.0625
- up_weight: bfloat16 [4, 7168, 1024], P('ep', 'sub'), may hold values from -0.0625 to 0.0625
- down_weight: bfloat16 [4, 1024, 7168], P('ep', None, 'sub'), may hold values from -0.1875 to 0.1875
- shared_gate: bfloat16 [1024, 7168], P('ep', 'sub'), may hold values from -0.0625 to 0.0625
- shared_up: bfloat16 [1024, 7168], P('ep', 'sub'), may hold values from -0.0625 to 0.0625
- shared_down: bfloat16 [1024, 7168], P('ep', 'sub'), may hold values from -0.1875 to 0.1875
Outputs:
- layer_out: bfloat16 [512, 7168], P(('groups', 'ep'), 'sub'), parts along dimension 0
There are 2 independent parts, one for each index of `groups`. A program takes and returns all parts, laid end to end along the dimension named above; an argument that names none is the same for every part. Nothing has to cross between parts.
Inputs may be any that keep to these rules, and one draw needn't show every extreme that they name: `expert_ids`: each row names 2 different experts. Among the 64 rows of one ep index no expert is named more than 48 times, and in some of these aligned blocks an expert is named exactly 48 times.
All inputs are finite; a program needn't handle non-finite values.
Results may differ from a plain program's by a relative error of at most 0.0054.
Values may be sent and summed in bfloat16 or wider, within the bound.
No kernel may reach another device: no remote copies, remote signals or barrier semaphores. Data moves between devices by JAX's collectives and lax.ppermute only.
A program may use at most 128 MiB of HBM per device.

v0:
```python
import jax
import jax.numpy as jnp
from jax import lax
from jax.sharding import PartitionSpec as P


def per_device(
    tokens,
    expert_ids,
    route_weights,
    gate_weight,
    up_weight,
    down_weight,
    shared_gate,
    shared_up,
    shared_down,
):
    contract = (((1,), (1,)), ((), ()))
    experts_all = lax.axis_size("ep")
    token_count = tokens.shape[0]
    quarter = tokens.shape[1]
    top_count = expert_ids.shape[1]
    capacity = token_count * top_count * 3 // (2 * experts_all)
    choices_flat = expert_ids.reshape(-1)
    one_hot = (choices_flat[:, None] == jnp.arange(experts_all, dtype=jnp.int32)[None, :]).astype(
        jnp.int32
    )
    earlier = jnp.cumsum(one_hot, axis=0) - one_hot
    slot_index = jnp.sum(earlier * one_hot, axis=1)
    target = choices_flat * capacity + slot_index
    target_grid = target.reshape(token_count, top_count)
    slot_ids = jnp.arange(experts_all * capacity, dtype=jnp.int32)
    placing = jnp.any(target_grid[None, :, :] == slot_ids[:, None, None], axis=2).astype(
        jnp.bfloat16
    )
    outgoing = jnp.dot(placing, tokens, preferred_element_type=jnp.float32).astype(jnp.bfloat16)
    outgoing = outgoing.reshape(experts_all, capacity, quarter)
    arrived = lax.all_to_all(outgoing, "ep", split_axis=0, concat_axis=0, tiled=True)
    expert_rows = arrived.reshape(-1, quarter)
    gate_part = jnp.dot(expert_rows, gate_weight[0], preferred_element_type=jnp.float32)
    up_part = jnp.dot(expert_rows, up_weight[0], preferred_element_type=jnp.float32)
    expert_pre, expert_lin = lax.psum((gate_part, up_part), "sub")
    expert_hidden = (jax.nn.silu(expert_pre) * expert_lin).astype(jnp.bfloat16)
    expert_out = jnp.dot(expert_hidden, down_weight[0], preferred_element_type=jnp.float32).astype(
        jnp.bfloat16
    )
    expert_out = expert_out.reshape(experts_all, capacity, quarter)
    returned = lax.all_to_all(expert_out, "ep", split_axis=0, concat_axis=0, tiled=True)
    gathered = returned.reshape(-1, quarter)[target].reshape(token_count, top_count, quarter)
    routed = jnp.sum(gathered.astype(jnp.float32) * route_weights[:, :, None], axis=1)
    local_width = shared_gate.shape[0]
    pieces_in = lax.all_gather(tokens, "ep", axis=0, tiled=True)
    gate_cols = lax.dot_general(
        pieces_in, shared_gate, contract, preferred_element_type=jnp.float32
    )
    up_cols = lax.dot_general(pieces_in, shared_up, contract, preferred_element_type=jnp.float32)
    combined = jnp.concatenate([gate_cols, up_cols], axis=1)
    combined = lax.psum(combined, "sub")
    shared_hidden = (jax.nn.silu(combined[:, :local_width]) * combined[:, local_width:]).astype(
        jnp.bfloat16
    )
    shared_out = lax.psum_scatter(
        jnp.dot(shared_hidden, shared_down, preferred_element_type=jnp.float32),
        "ep",
        scatter_dimension=0,
        tiled=True,
    )
    return (shared_out + routed).astype(jnp.bfloat16)


def solution(mesh):
    in_specs = (
        P(("groups", "ep"), "sub"),
        P(("groups", "ep"), None),
        P(("groups", "ep"), None),
        P("ep", "sub", None),
        P("ep", "sub", None),
        P("ep", None, "sub"),
        P("ep", "sub"),
        P("ep", "sub"),
        P("ep", "sub"),
    )
    out_specs = P(("groups", "ep"), "sub")
    return jax.shard_map(
        per_device, mesh=mesh, in_specs=in_specs, out_specs=out_specs, check_vma=False
    )
```

profile of v0, /device:TPU:8, one launch (start us, length us, event | category | flops | bytes accessed | tf_op | source)
XLA Modules:
  0.0 173.0 jit_solution(14425306937453339064)
XLA Ops:
  6.5 0.0 copy-start
  6.5 0.0 copy-start.2
  6.5 0.0 copy-start.3
  6.5 0.9 copy.16
  7.5 0.1 eq.28
  7.6 0.1 fusion.15
  7.7 0.2 reduce_window_sum.11
  7.9 0.2 select_reduce_fusion
  8.0 0.1 reduce_sum.23
  8.2 0.1 copy.18
  8.3 0.1 fusion.14
  8.4 2.2 %convolution_convert_fusion = bf16[192,1792]{1,0:T(8,128)(2,1)} fusion(pred[192,64]{0,1:T(8,128)(4,1)S(1)} %fusion.14, bf16[64,1792]{1,0:T(8,128)(2,1)} %param.9), kind=kOutput, calls=%fused_computation.8 | convolution fusion | flops 44384256 | bytes 929792 | tf_op jit(solution)/shard_map/dot_general | solution.py:36
  10.6 5.3 %all-to-all-start = ((bf16[4,48,1792]{2,1,0:T(8,128)(2,1)}), bf16[4,48,1792]{2,1,0:T(8,128)(2,1)S(1)}, u32[]{:S(2)}, u32[]{:S(2)}) async-start(bf16[4,48,1792]{2,1,0:T(8,128)(2,1)} %bitcast), calls=%async_computation.1 | async-start | bytes 1376256 | tf_op jit(solution)/shard_map/all_to_all | solution.py:38
  15.9 0.0 all-reduce.3.cloned.1.call-start
  15.9 32.0 %all_gather.3 = bf16[256,1792]{1,0:T(8,128)(2,1)S(1)} all-gather(bf16[64,1792]{1,0:T(8,128)(2,1)} %param.9), channel_id=1, replica_groups=mesh['groups'=2,'ep'=4,'sub'=4] {'ep'}, dimensions={0}, use_global_device_ids=true | all-gather | bytes 1146880 | tf_op jit(solution)/shard_map/all_gather | solution.py:52
  47.9 0.0 copy-done.2
  47.9 0.4 fusion.20
  48.3 0.0 copy-done.3
  48.3 0.4 fusion.21
  48.8 0.8 pad_maximum_fusion
  49.6 0.0 all-to-all-done
  49.6 0.0 copy-start.1
  49.6 4.0 %fusion.2 = f32[192,1024]{1,0:T(8,128)} fusion(bf16[192,1792]{1,0:T(8,128)(2,1)S(1)} %bitcast.31, bf16[1,1792,1024]{2,1,0:T(8,128)(2,1)} %param.13), kind=kOutput, calls=%fused_computation.3 | convolution fusion | flops 704643072 | bytes 5144576 | tf_op jit(solution)/shard_map/dot_general | solution.py:41
  53.6 0.0 copy-done.1
  53.6 1.8 %fusion.4 = f32[192,1024]{1,0:T(8,128)} fusion(bf16[192,1792]{1,0:T(8,128)(2,1)S(1)} %bitcast.32, bf16[1,1792,1024]{2,1,0:T(8,128)(2,1)S(1)} %copy-done.1), kind=kOutput, calls=%fused_computation.5 | convolution fusion | flops 704643072 | bytes 5144576 | tf_op jit(solution)/shard_map/dot_general | solution.py:40
  55.4 0.0 all-reduce.3.cloned.1.call-update
  55.4 0.0 reduce-scatter.2.cloned.1.call-start
  55.5 52.5 %all-reduce.3.cloned.1.call-done = (f32[192,1024]{1,0:T(8,128)}, f32[192,1024]{1,0:T(8,128)}, f32[256,512]{0,1:T(8,128)}) async-done(((f32[192,1024]{1,0:T(8,128)}, f32[192,1024]{1,0:T(8,128)}, f32[256,512]{0,1:T(8,128)}), (f32[192,1024]{1,0:T(8,128)}, f32[192,1024]{1,0:T(8,128)}, f32[256,512]{0,1:T(8,128)})) %all-reduce.3.cloned.1.call-update) | async-done | bytes 2097168 | tf_op jit(solution)/shard_map/psum | solution.py:42
  107.9 0.0 copy-start.5
  107.9 0.0 copy-start.6
  107.9 0.0 copy-done
  107.9 2.9 %fusion.11 = f32[256,1792]{1,0:T(8,128)} fusion(bf16[256,1792]{1,0:T(8,128)(2,1)S(1)} %copy-done, f32[256,512]{0,1:T(8,128)} %get-tuple-element.7), kind=kOutput, calls=%fused_computation.16 | convolution fusion | flops 235274240 | bytes 3276800 | tf_op jit(solution)/shard_map/dot_general | solution.py:63
  110.8 0.0 reduce-scatter.2.cloned.1.call-update
  110.8 0.0 copy-done.5
  110.9 0.0 copy-done.6
  110.9 0.0 copy-start.4
  110.9 3.9 %fusion.6 = bf16[192,1792]{1,0:T(8,128)(2,1)} fusion(bf16[1,1024,1792]{2,1,0:T(8,128)(2,1)} %param.14, f32[192,1024]{1,0:T(8,128)S(1)} %copy-done.5, f32[192,1024]{1,0:T(8,128)S(1)} %copy-done.6), kind=kOutput, calls=%fused_computation.7 | convolution fusion | flops 706166784 | bytes 5931008 | tf_op jit(solution)/shard_map/dot_general | solution.py:44
  114.8 5.1 %all-to-all-start.1 = ((bf16[4,48,1792]{2,1,0:T(8,128)(2,1)}), bf16[4,48,1792]{2,1,0:T(8,128)(2,1)S(1)}, u32[]{:S(2)}, u32[]{:S(2)}) async-start(bf16[4,48,1792]{2,1,0:T(8,128)(2,1)} %bitcast.5), calls=%async_computation.2 | async-start | bytes 1376256 | tf_op jit(solution)/shard_map/all_to_all | solution.py:48
  119.9 0.1 mul.50
  120.1 0.0 copy-done.4
  120.1 0.1 copy.19
  120.2 33.8 %all-to-all-done.1 = bf16[4,48,1792]{2,1,0:T(8,128)(2,1)S(1)} async-done(((bf16[4,48,1792]{2,1,0:T(8,128)(2,1)}), bf16[4,48,1792]{2,1,0:T(8,128)(2,1)S(1)}, u32[]{:S(2)}, u32[]{:S(2)}) %all-to-all-start.1) | async-done | bytes 688160 | tf_op jit(solution)/shard_map/all_to_all | solution.py:48
  154.0 0.9 gather_fusion
  154.9 0.4 reshape.56
  155.4 1.3 multiply_reduce_fusion
  156.7 7.7 %reduce-scatter.2.cloned.1.call-done = f32[64,1792]{1,0:T(8,128)} async-done(((f32[256,1792]{1,0:T(8,128)}), f32[64,1792]{1,0:T(8,128)}) %reduce-scatter.2.cloned.1.call-update) | async-done | bytes 458768 | tf_op jit(solution)/shard_map/reduce_scatter | solution.py:62
  164.4 1.8 %add_convert_fusion = bf16[64,1792]{1,0:T(8,128)(2,1)} fusion(f32[64,1792]{1,0:T(8,128)} %reduce-scatter.2.cloned.1.call-done, f32[64,1792]{1,0:T(8,128)S(1)} %multiply_reduce_fusion), kind=kLoop, calls=%fused_computation.12 | loop fusion | flops 229376 | bytes 1146880 | tf_op jit(solution)/shard_map/convert_element_type | solution.py:68
  (3 shorter events, 0.0 us)
Async XLA Ops:
  6.5 101.4 %copy-start = (bf16[256,1792]{1,0:T(8,128)(2,1)S(1)}, bf16[256,1792]{1,0:T(8,128)(2,1)}, u32[]{:S(2)}) copy-start(bf16[256,1792]{1,0:T(8,128)(2,1)} %param.17) | copy-start | bytes 2752516
  6.5 41.3 %copy-start.2 = (bf16[256,1792]{1,0:T(8,128)(2,1)S(1)}, bf16[256,1792]{1,0:T(8,128)(2,1)}, u32[]{:S(2)}) copy-start(bf16[256,1792]{1,0:T(8,128)(2,1)} %param.15) | copy-start | bytes 2752516
  6.5 41.8 %copy-start.3 = (bf16[256,1792]{1,0:T(8,128)(2,1)S(1)}, bf16[256,1792]{1,0:T(8,128)(2,1)}, u32[]{:S(2)}) copy-start(bf16[256,1792]{1,0:T(8,128)(2,1)} %param.16) | copy-start | bytes 2752516
  10.6 39.0 %all-to-all-start = ((bf16[4,48,1792]{2,1,0:T(8,128)(2,1)}), bf16[4,48,1792]{2,1,0:T(8,128)(2,1)S(1)}, u32[]{:S(2)}, u32[]{:S(2)}) async-start(bf16[4,48,1792]{2,1,0:T(8,128)(2,1)} %bitcast), calls=%async_computation.1 | async-start | bytes 1376256 | tf_op jit(solution)/shard_map/all_to_all | solution.py:38
  15.9 92.0 %all-reduce.3.cloned.1.call-start = ((), (), s32[]{:S(2)}) async-start(), calls=%async_computation.4 | async-start | bytes 4194304 | tf_op jit(solution)/shard_map/psum | solution.py:42
  49.6 4.0 %copy-start.1 = (bf16[1,1792,1024]{2,1,0:T(8,128)(2,1)S(1)}, bf16[1,1792,1024]{2,1,0:T(8,128)(2,1)}, u32[]{:S(2)}) copy-start(bf16[1,1792,1024]{2,1,0:T(8,128)(2,1)} %param.12) | copy-start | bytes 11010052
  55.4 109.0 %reduce-scatter.2.cloned.1.call-start = ((), (), s32[]{:S(2)}) async-start(), calls=%async_computation.3 | async-start | bytes 2293760 | tf_op jit(solution)/shard_map/reduce_scatter | solution.py:62
  107.9 2.9 %copy-start.5 = (f32[192,1024]{1,0:T(8,128)S(1)}, f32[192,1024]{1,0:T(8,128)}, u32[]{:S(2)}) copy-start(f32[192,1024]{1,0:T(8,128)} %get-tuple-element.5) | copy-start | bytes 2359300
  107.9 2.9 %copy-start.6 = (f32[192,1024]{1,0:T(8,128)S(1)}, f32[192,1024]{1,0:T(8,128)}, u32[]{:S(2)}) copy-start(f32[192,1024]{1,0:T(8,128)} %get-tuple-element.6) | copy-start | bytes 2359300
  110.9 9.2 %copy-start.4 = (f32[64,2]{0,1:T(2,128)S(1)}, f32[64,2]{0,1:T(2,128)}, u32[]{:S(2)}) copy-start(f32[64,2]{0,1:T(2,128)} %param.11) | copy-start | bytes 1540
  114.8 39.2 %all-to-all-start.1 = ((bf16[4,48,1792]{2,1,0:T(8,128)(2,1)}), bf16[4,48,1792]{2,1,0:T(8,128)(2,1)S(1)}, u32[]{:S(2)}, u32[]{:S(2)}) async-start(bf16[4,48,1792]{2,1,0:T(8,128)(2,1)} %bitcast.5), calls=%async_computation.2 | async-start | bytes 1376256 | tf_op jit(solution)/shard_map/all_to_all | solution.py:48
Sparse Core Ops, SparseCore 0:
  55.5 52.3 all-reduce.2
  111.0 53.3 reduce-scatter.1
where the time goes:
time: 173 us
  waiting for transfers between devices  94 us (54%)
  blocking collectives  32 us (18%)
  matrix products  15.7 us (9%)
  between operations  13.5 us (8%)
  starting transfers between devices  10.5 us (6%)
  other arithmetic  4.46 us (3%)
  local copies, waits for them, and re-layouts  2.9 us (2%)
    psum x1, waiting for transfers between devices, per_device(): expert_pre, expert_lin = lax.psum((gate_part, up_part), 'sub')  52.5 us
    all_to_all x1, waiting for transfers between devices, per_device(): lax.all_to_all(expert_out, 'ep', split_axis=0, concat_axis=0, tiled=True)  33.8 us
    all_gather x1, blocking collectives, per_device(): pieces_in = lax.all_gather(tokens, 'ep', axis=0, tiled=True)  32 us
    reduce_scatter x1, waiting for transfers between devices, per_device(): lax.psum_scatter(jnp.dot(shared_hidden, shared_down, preferred_element_ty...  7.73 us
    all_to_all x1, starting transfers between devices, per_device(): lax.all_to_all(outgoing, 'ep', split_axis=0, concat_axis=0, tiled=True)  5.32 us
    all_to_all x1, starting transfers between devices, per_device(): lax.all_to_all(expert_out, 'ep', split_axis=0, concat_axis=0, tiled=True)  5.13 us
    dot_general x1, matrix products, per_device(): jnp.dot(expert_rows, up_weight[0], preferred_element_type=jnp.float32)  4 us
    dot_general x1, matrix products, per_device(): jnp.dot(expert_hidden, down_weight[0], preferred_element_type=jnp.float32)  3.9 us
  transfers between devices with their start and end apart: 4, of which 3 were waited for; matrix products, arithmetic and copies ran while one was open for 5% of the time, Pallas kernels for 0%

commit v1 on v0

v1 whole, which is shorter than its diff:
```python
import jax
import jax.numpy as jnp
from jax import lax
from jax.sharding import PartitionSpec as P

WIRE = jnp.bfloat16
TOTAL = jnp.float32


def turn(value, axis, by):
    size = lax.axis_size(axis)
    return lax.ppermute(value, axis, [(i, (i + by) % size) for i in range(size)])


def swap(value, axis, bit):
    size = lax.axis_size(axis)
    return lax.ppermute(value, axis, [(i, i ^ bit) for i in range(size)])


def summed_rows(part):
    size, me = lax.axis_size("sub"), lax.axis_index("sub")
    bit = 1
    while bit * 2 < size:
        half = part.shape[0] // 2
        upper = (me & bit) != 0
        low, high = part[:half], part[half:]
        sent = jnp.where(upper, low, high).astype(WIRE)
        part = jnp.where(upper, high, low) + swap(sent, "sub", bit).astype(TOTAL)
        bit *= 2
    if bit < size:
        part = part + swap(part.astype(WIRE), "sub", bit).astype(TOTAL)
    return part


def gathered_rows(share):
    size, me = lax.axis_size("sub"), lax.axis_index("sub")
    bits = []
    b = 1
    while b * 2 < size:
        bits.append(b)
        b *= 2
    for b in reversed(bits):
        other = swap(share, "sub", b)
        upper = (me & b) != 0
        share = jnp.where(
            upper, jnp.concatenate([other, share]), jnp.concatenate([share, other])
        )
    return share


def per_device(
    tokens,
    expert_ids,
    route_weights,
    gate_weight,
    up_weight,
    down_weight,
    shared_gate,
    shared_up,
    shared_down,
):
    contract = (((1,), (1,)), ((), ()))
    experts = lax.axis_size("ep")
    me = lax.axis_index("ep")
    count = tokens.shape[0]
    hidden, narrow = gate_weight.shape[2], shared_gate.shape[0]
    blocks = [tokens] + [turn(tokens, "ep", k) for k in range(1, experts)]
    named = expert_ids[:, :, None] == jnp.arange(experts, dtype=jnp.int32)
    dense = jnp.sum(jnp.where(named, route_weights[:, :, None], 0.0), axis=1)
    scales = lax.all_gather(dense.T, "ep", axis=1, tiled=False)[me]
    chunks = [[0]] + [
        sorted({k, experts - k}) for k in range(1, experts // 2 + 1)
    ]
    answers = []
    for chunk in chunks:
        rows = jnp.concatenate([blocks[k] for k in chunk])
        parts = [
            jnp.dot(rows, gate_weight[0], preferred_element_type=TOTAL),
            jnp.dot(rows, up_weight[0], preferred_element_type=TOTAL),
            lax.dot_general(rows, shared_gate, contract, preferred_element_type=TOTAL),
            lax.dot_general(rows, shared_up, contract, preferred_element_type=TOTAL),
        ]
        full = summed_rows(jnp.concatenate(parts, axis=1))
        pre, lin = full[:, :hidden], full[:, hidden : 2 * hidden]
        pre_s, lin_s = full[:, 2 * hidden : -narrow], full[:, -narrow:]
        act = jnp.concatenate(
            [jax.nn.silu(pre) * lin, jax.nn.silu(pre_s) * lin_s], axis=1
        ).astype(jnp.bfloat16)
        act = gathered_rows(act)
        scale = jnp.concatenate([scales[(me - k) % experts] for k in chunk])
        out = jnp.dot(act[:, hidden:], shared_down, preferred_element_type=TOTAL)
        out = out + scale[:, None] * jnp.dot(
            act[:, :hidden], down_weight[0], preferred_element_type=TOTAL
        )
        for place, k in enumerate(chunk):
            piece = out[place * count : (place + 1) * count]
            answers.append(piece if k == 0 else turn(piece.astype(WIRE), "ep", -k))
    total = answers[0]
    for answer in answers[1:]:
        total = total + answer.astype(TOTAL)
    return total.astype(jnp.bfloat16)


def solution(mesh):
    in_specs = (
        P(("groups", "ep"), "sub"),
        P(("groups", "ep"), None),
        P(("groups", "ep"), None),
        P("ep", "sub", None),
        P("ep", "sub", None),
        P("ep", None, "sub"),
        P("ep", "sub"),
        P("ep", "sub"),
        P("ep", "sub"),
    )
    out_specs = P(("groups", "ep"), "sub")
    return jax.shard_map(
        per_device, mesh=mesh, in_specs=in_specs, out_specs=out_specs, check_vma=False
    )
```

time: 173 us -> 88.2 us (0.51)
  waiting for transfers between devices: 94 us -> 30.7 us
  blocking collectives: 32 us -> 13.3 us
  between operations: 13.5 us -> 0.38 us
  matrix products: 15.7 us -> 20.2 us
  starting transfers between devices: 10.5 us -> 14.2 us
    psum x1 -> x0, waiting for transfers between devices: 52.5 us -> none  [per_device(): expert_pre, expert_lin = lax.psum((gate_part, up_part), 'sub')]
    all_to_all x2 -> x0, waiting for transfers between devices: 33.8 us -> none  [the longest x1 33.8 us: per_device(): lax.all_to_all(expert_out, 'ep', split_axis=0, concat_axis=0, tiled=True)]
    ppermute x0 -> x15, waiting for transfers between devices: none -> 30.7 us  [the longest x6 16.3 us: turn(): lax.ppermute(value, axis, [(i, (i + by) % size) for i in range(size)])]
    all_gather x1, blocking collectives: 32 us -> 13.3 us  [per_device(): scales = lax.all_gather(dense.T, 'ep', axis=1, tiled=False)[me]]
    ppermute x0 -> x15, starting transfers between devices: none -> 14.2 us  [the longest x6 10.7 us: turn(): lax.ppermute(value, axis, [(i, (i + by) % size) for i in range(size)])]
    all_to_all x2 -> x0, starting transfers between devices: 10.4 us -> none  [the longest x1 5.32 us: per_device(): lax.all_to_all(outgoing, 'ep', split_axis=0, concat_axis=0, tiled=True)]
    reduce_scatter x1 -> x0, waiting for transfers between devices: 7.73 us -> none  [per_device(): lax.psum_scatter(jnp.dot(shared_hidden, shared_down, preferred_element_ty...]
    dot_general x7 -> x18, matrix products: 15.7 us -> 20.2 us  [the longest x3 6.17 us: per_device(): jnp.dot(rows, up_weight[0], preferred_element_type=TOTAL)]
  transfers between devices with their start and end apart: 4 -> 15, of which waited for: 3 -> 6; matrix products, arithmetic and copies ran while one was open for 5% -> 30% of each run, Pallas kernels for 0% -> 0%
where the time goes in v1:
time: 88.2 us; the launch traced here: 86.9 us
  waiting for transfers between devices  30.7 us (35%)
  matrix products  20.2 us (23%)
  starting transfers between devices  14.2 us (16%)
  blocking collectives  13.3 us (15%)
  other arithmetic  5.14 us (6%)
  local copies, waits for them, and re-layouts  3.02 us (3%)
    ppermute x6, waiting for transfers between devices, turn(): lax.ppermute(value, axis, [(i, (i + by) % size) for i in range(size)])  16.3 us
    ppermute x9, waiting for transfers between devices, swap(): return lax.ppermute(value, axis, [(i, i ^ bit) for i in range(size)])  14.4 us
    all_gather x1, blocking collectives, per_device(): scales = lax.all_gather(dense.T, 'ep', axis=1, tiled=False)[me]  13.3 us
    ppermute x6, starting transfers between devices, turn(): lax.ppermute(value, axis, [(i, (i + by) % size) for i in range(size)])  10.7 us
    dot_general x3, matrix products, per_device(): jnp.dot(rows, up_weight[0], preferred_element_type=TOTAL)  6.17 us
    dot_general x3, matrix products, per_device(): jnp.dot(rows, gate_weight[0], preferred_element_type=TOTAL)  5.85 us
    ppermute x9, starting transfers between devices, swap(): return lax.ppermute(value, axis, [(i, i ^ bit) for i in range(size)])  3.57 us
    dot_general x3, matrix products, per_device(): lax.dot_general(rows, shared_up, contract, preferred_element_type=TOTAL)  2.23 us
  transfers between devices with their start and end apart: 15, of which 6 were waited for; matrix products, arithmetic and copies ran while one was open for 30% of the time, Pallas kernels for 0%

profile of v1, /device:TPU:8, one launch (start us, length us, event | category | flops | bytes accessed | tf_op | source)
XLA Modules:
  0.0 86.9 jit_solution(8689166936966970250)
XLA Ops:
  0.0 1.6 %collective-permute-start.3 = (bf16[64,1792]{1,0:T(8,128)(2,1)}, bf16[64,1792]{1,0:T(8,128)(2,1)}, u32[]{:S(2)}, u32[]{:S(2)}) collective-permute-start(bf16[64,1792]{1,0:T(8,128)(2,1)} %param.9), channel_id=1, source_target_pairs={{0,4},{4,8},{8,12},{12,0},{1,5},{5,9},{9,13},{13,1},{2,6},{6,10},{... | collective-permute-start | bytes 688136 | tf_op jit(solution)/shard_map/ppermute | solution.py:12
  1.6 0.4 collective-permute-start.4
  2.0 2.6 %collective-permute-start.10 = (bf16[64,1792]{1,0:T(8,128)(2,1)}, bf16[64,1792]{1,0:T(8,128)(2,1)}, u32[]{:S(2)}, u32[]{:S(2)}) collective-permute-start(bf16[64,1792]{1,0:T(8,128)(2,1)} %param.9), channel_id=1, source_target_pairs={{0,8},{4,12},{8,0},{12,4},{1,9},{5,13},{9,1},{13,5},{2,10},{6,14},... | collective-permute-start | bytes 688136 | tf_op jit(solution)/shard_map/ppermute | solution.py:12
  4.6 3.8 %fusion.10 = f32[64,1024]{1,0:T(8,128)} fusion(bf16[64,1792]{1,0:T(8,128)(2,1)} %param.9, bf16[1,1792,1024]{2,1,0:T(8,128)(2,1)} %param.13), kind=kOutput, calls=%fused_computation.10 | convolution fusion | flops 234881024 | bytes 4161536 | tf_op jit(solution)/shard_map/dot_general | solution.py:79
  8.4 1.5 %fusion.16 = f32[64,1024]{1,0:T(8,128)} fusion(bf16[64,1792]{1,0:T(8,128)(2,1)S(1)} %copy-done.7, bf16[1,1792,1024]{2,1,0:T(8,128)(2,1)S(1)} %copy-done.2), kind=kOutput, calls=%fused_computation.16 | convolution fusion | flops 234881024 | bytes 4161536 | tf_op jit(solution)/shard_map/dot_general | solution.py:78
  9.9 0.4 fusion.53
  10.3 0.4 fusion.54
  10.7 1.1 %pad_maximum_fusion.1 = f32[64,2560]{1,0:T(8,128)S(1)} fusion(f32[64,256]{1,0:T(8,128)S(1)} %fusion.54, f32[64,256]{1,0:T(8,128)S(1)} %fusion.53, f32[64,1024]{1,0:T(8,128)} %fusion.10, f32[64,1024]{1,0:T(8,128)} %fusion.16), kind=kLoop, calls=%fused_computation.31 | loop fusion | flops 491520 | bytes 1310720 | tf_op jit(solution)/shard_map/concatenate | solution.py:83
  11.8 0.7 select_convert_fusion.2
  12.6 13.3 %all-gather.1 = f32[4,64,4]{1,2,0:T(4,128)S(1)} all-gather(f32[1,64,4]{1,2,0:T(4,128)S(1)} %bitcast.61), channel_id=2, replica_groups=mesh['groups'=2,'ep'=4,'sub'=4] {'ep'}, dimensions={0}, use_global_device_ids=true | all-gather | bytes 5120 | tf_op jit(solution)/shard_map/all_gather | solution.py:70
  25.8 0.1 reshape.15
  25.9 0.1 reshape.13
  26.1 1.1 %fusion.46 = bf16[32,2560]{1,0:T(8,128)(2,1)S(1)} fusion(bf16[32,2560]{1,0:T(8,128)(2,1)} %collective-permute-done, f32[64,2560]{1,0:T(8,128)S(1)} %pad_maximum_fusion.1, pred[]{:T(512)S(6)} %ne.26), kind=kLoop, calls=%fused_computation.71 | loop fusion | flops 327680 | bytes 983041 | tf_op jit(solution)/shard_map/convert_element_type | solution.py:31
  27.2 1.6 %collective-permute-start.1 = (bf16[32,2560]{1,0:T(8,128)(2,1)S(1)}, bf16[32,2560]{1,0:T(8,128)(2,1)S(1)}, u32[]{:S(2)}, u32[]{:S(2)}) collective-permute-start(bf16[32,2560]{1,0:T(8,128)(2,1)S(1)} %fusion.46), channel_id=1, source_target_pairs={{0,2},{1,3},{2,0},{3,1},{4,6},{5,7},{6,4},{7,5},{8,10},{9,11},{10,... | collective-permute-start | bytes 491528 | tf_op jit(solution)/shard_map/ppermute | solution.py:17
  28.8 1.0 %constant_dynamic-update-slice_fusion.1 = bf16[128,1792]{1,0:T(8,128)(2,1)S(1)} fusion(bf16[64,1792]{1,0:T(8,128)(2,1)} %collective-permute-done.3), kind=kLoop, calls=%fused_computation.68 | loop fusion | bytes 458752
  29.7 1.0 %constant_dynamic-update-slice_fusion = bf16[128,1792]{1,0:T(8,128)(2,1)S(1)} fusion(bf16[128,1792]{1,0:T(8,128)(2,1)S(1)} %constant_dynamic-update-slice_fusion.1, bf16[64,1792]{1,0:T(8,128)(2,1)} %collective-permute-done.4), kind=kLoop, calls=%fused_computation.67 | loop fusion | bytes 458752 | tf_op jit(solution)/shard_map/concatenate | solution.py:76
  30.7 2.7 %fusion.14 = f32[128,1024]{1,0:T(8,128)S(1)} fusion(bf16[128,1792]{1,0:T(8,128)(2,1)S(1)} %constant_dynamic-update-slice_fusion, bf16[1,1792,1024]{2,1,0:T(8,128)(2,1)} %param.12), kind=kOutput, calls=%fused_computation.14 | convolution fusion | flops 469762048 | bytes 4653056 | tf_op jit(solution)/shard_map/dot_general | solution.py:78
  33.4 0.7 fusion.8
  34.1 0.5 fusion.55
  34.6 0.5 fusion.56
  35.0 0.1 pad_maximum_fusion
  35.3 0.8 copy-done.3
  36.1 1.7 %fusion.12 = f32[64,1024]{1,0:T(8,128)S(1)} fusion(bf16[64,1792]{1,0:T(8,128)(2,1)} %collective-permute-done.10, bf16[1,1792,1024]{2,1,0:T(8,128)(2,1)S(1)} %copy-done.3), kind=kOutput, calls=%fused_computation.12 | convolution fusion | flops 234881024 | bytes 4161536 | tf_op jit(solution)/shard_map/dot_general | solution.py:78
  37.8 1.7 %fusion.6 = f32[64,1024]{1,0:T(8,128)S(1)} fusion(bf16[64,1792]{1,0:T(8,128)(2,1)} %collective-permute-done.10, bf16[1,1792,1024]{2,1,0:T(8,128)(2,1)S(1)} %copy-done.4), kind=kOutput, calls=%fused_computation.6 | convolution fusion | flops 234881024 | bytes 4161536 | tf_op jit(solution)/shard_map/dot_general | solution.py:79
  39.6 1.3 %fusion.57 = f32[64,256]{1,0:T(8,128)S(1)} fusion(bf16[64,1792]{1,0:T(8,128)(2,1)} %collective-permute-done.10, bf16[256,1792]{1,0:T(8,128)(2,1)S(1)} %copy-done.5), kind=kOutput, calls=%fused_computation.87 | convolution fusion | flops 58720256 | bytes 1212416 | tf_op jit(solution)/shard_map/dot_general | solution.py:80
  40.9 1.4 %fusion.58 = f32[64,256]{1,0:T(8,128)S(1)} fusion(bf16[64,1792]{1,0:T(8,128)(2,1)} %collective-permute-done.10, bf16[256,1792]{1,0:T(8,128)(2,1)S(1)} %copy-done.6), kind=kOutput, calls=%fused_computation.88 | convolution fusion | flops 58720256 | bytes 1212416 | tf_op jit(solution)/shard_map/dot_general | solution.py:81
  42.5 1.1 %convert_add_fusion.4 = f32[32,2560]{1,0:T(8,128)S(1)} fusion(bf16[32,2560]{1,0:T(8,128)(2,1)S(1)} %collective-permute-done.1, bf16[32,2560]{1,0:T(8,128)(2,1)} %collective-permute-done, f32[64,2560]{1,0:T(8,128)S(1)} %pad_maximum_fusion.1, pred[]{:T(512)S(6)} %ne.26), kind=kLoop, calls=%fused_computation.40 | loop fusion | flops 409600 | bytes 1310721 | tf_op jit(solution)/shard_map/add | solution.py:31
  43.7 0.6 collective-permute-start.2
  44.3 0.6 collective-permute-start.12
  44.9 0.3 collective-permute-done.2
  45.2 5.3 %collective-permute-done.12 = bf16[32,2560]{1,0:T(8,128)(2,1)S(1)} collective-permute-done((bf16[32,2560]{1,0:T(8,128)(2,1)S(1)}, bf16[32,2560]{1,0:T(8,128)(2,1)S(1)}, u32[]{:S(2)}, u32[]{:S(2)}) %collective-permute-start.12) | collective-permute-done | bytes 163872 | tf_op jit(solution)/shard_map/ppermute | solution.py:17
  50.8 0.1 fusion.45
  50.9 0.6 collective-permute-start.6
  51.5 0.6 collective-permute-done.13
  52.1 0.7 fusion.25
  52.8 8.2 %collective-permute-done.6 = bf16[64,2560]{1,0:T(8,128)(2,1)S(1)} collective-permute-done((bf16[64,2560]{1,0:T(8,128)(2,1)S(1)}, bf16[64,2560]{1,0:T(8,128)(2,1)S(1)}, u32[]{:S(2)}, u32[]{:S(2)}) %collective-permute-start.6) | collective-permute-done | bytes 327712 | tf_op jit(solution)/shard_map/ppermute | solution.py:17
  61.1 0.1 convert_add_fusion
  61.2 0.1 fusion.34
  61.5 0.3 fusion.32
  61.7 3.1 %collective-permute-start.14 = (bf16[64,1792]{1,0:T(8,128)(2,1)S(1)}, bf16[64,1792]{1,0:T(8,128)(2,1)S(1)}, u32[]{:S(2)}, u32[]{:S(2)}) collective-permute-start(bf16[64,1792]{1,0:T(8,128)(2,1)S(1)} %fusion.32), channel_id=1, source_target_pairs={{0,8},{4,12},{8,0},{12,4},{1,9},{5,13},{9,1},{13,5},{2,10},{6,14},... | collective-permute-start | bytes 688136 | tf_op jit(solution)/shard_map/ppermute | solution.py:12
  64.9 0.7 fusion.18
  65.6 0.3 fusion.21
  65.9 2.4 %collective-permute-start.8 = (bf16[64,1792]{1,0:T(8,128)(2,1)S(1)}, bf16[64,1792]{1,0:T(8,128)(2,1)S(1)}, u32[]{:S(2)}, u32[]{:S(2)}) collective-permute-start(bf16[64,1792]{1,0:T(8,128)(2,1)S(1)} %get-tuple-element.5), channel_id=1, source_target_pairs={{0,12},{4,0},{8,4},{12,8},{1,13},{5,1},{9,5},{13,9},{2,14},{6,2},{... | collective-permute-start | bytes 688136 | tf_op jit(solution)/shard_map/ppermute | solution.py:12
  68.3 0.5 collective-permute-start.9
  68.9 0.7 fusion.22
  69.6 11.1 %collective-permute-done.14 = bf16[64,1792]{1,0:T(8,128)(2,1)S(1)} collective-permute-done((bf16[64,1792]{1,0:T(8,128)(2,1)S(1)}, bf16[64,1792]{1,0:T(8,128)(2,1)S(1)}, u32[]{:S(2)}, u32[]{:S(2)}) %collective-permute-start.14) | collective-permute-done | bytes 229408 | tf_op jit(solution)/shard_map/ppermute | solution.py:12
  80.7 5.2 %collective-permute-done.8 = bf16[64,1792]{1,0:T(8,128)(2,1)S(1)} collective-permute-done((bf16[64,1792]{1,0:T(8,128)(2,1)S(1)}, bf16[64,1792]{1,0:T(8,128)(2,1)S(1)}, u32[]{:S(2)}, u32[]{:S(2)}) %collective-permute-start.8) | collective-permute-done | bytes 229408 | tf_op jit(solution)/shard_map/ppermute | solution.py:12
  85.9 1.0 %fusion.31 = bf16[64,1792]{1,0:T(8,128)(2,1)} fusion(f32[64,1792]{1,0:T(8,128)S(1)} %fusion.22, bf16[256,1792]{1,0:T(8,128)(2,1)S(1)} %copy-done, bf16[64,1792]{1,0:T(8,128)(2,1)S(1)} %collective-permute-done.14, bf16[64,1792]{1,0:T(8,128)(2,1)S(1)} %collective-permute-done.9, bf16[64,1792]{1,0:T(8,128)(2,1)S(1)} %collective-permute-done.8, ...), kind=kOutput, calls=%fused_computation.28 | convolution fusion | flops 59637760 | bytes 2326528 | tf_op jit(solution)/shard_map/dot_general | solution.py:91
  (54 shorter events, 1.1 us)
Async XLA Ops:
  0.0 61.5 %copy-start = (bf16[256,1792]{1,0:T(8,128)(2,1)S(1)}, bf16[256,1792]{1,0:T(8,128)(2,1)}, u32[]{:S(2)}) copy-start(bf16[256,1792]{1,0:T(8,128)(2,1)} %param.17) | copy-start | bytes 2752516
  0.0 8.4 %copy-start.7 = (bf16[64,1792]{1,0:T(8,128)(2,1)S(1)}, bf16[64,1792]{1,0:T(8,128)(2,1)}, u32[]{:S(2)}) copy-start(bf16[64,1792]{1,0:T(8,128)(2,1)} %param.9) | copy-start | bytes 688132
  0.0 28.8 %collective-permute-start.3 = (bf16[64,1792]{1,0:T(8,128)(2,1)}, bf16[64,1792]{1,0:T(8,128)(2,1)}, u32[]{:S(2)}, u32[]{:S(2)}) collective-permute-start(bf16[64,1792]{1,0:T(8,128)(2,1)} %param.9), channel_id=1, source_target_pairs={{0,4},{4,8},{8,12},{12,0},{1,5},{5,9},{9,13},{13,1},{2,6},{6,10},{... | collective-permute-start | bytes 688136 | tf_op jit(solution)/shard_map/ppermute | solution.py:12
  1.6 28.1 %collective-permute-start.4 = (bf16[64,1792]{1,0:T(8,128)(2,1)}, bf16[64,1792]{1,0:T(8,128)(2,1)}, u32[]{:S(2)}, u32[]{:S(2)}) collective-permute-start(bf16[64,1792]{1,0:T(8,128)(2,1)} %param.9), channel_id=1, source_target_pairs={{0,12},{4,0},{8,4},{12,8},{1,13},{5,1},{9,5},{13,9},{2,14},{6,2},{... | collective-permute-start | bytes 688136 | tf_op jit(solution)/shard_map/ppermute | solution.py:12
  2.0 33.3 %collective-permute-start.10 = (bf16[64,1792]{1,0:T(8,128)(2,1)}, bf16[64,1792]{1,0:T(8,128)(2,1)}, u32[]{:S(2)}, u32[]{:S(2)}) collective-permute-start(bf16[64,1792]{1,0:T(8,128)(2,1)} %param.9), channel_id=1, source_target_pairs={{0,8},{4,12},{8,0},{12,4},{1,9},{5,13},{9,1},{13,5},{2,10},{6,14},... | collective-permute-start | bytes 688136 | tf_op jit(solution)/shard_map/ppermute | solution.py:12
  4.6 3.8 %copy-start.2 = (bf16[1,1792,1024]{2,1,0:T(8,128)(2,1)S(1)}, bf16[1,1792,1024]{2,1,0:T(8,128)(2,1)}, u32[]{:S(2)}) copy-start(bf16[1,1792,1024]{2,1,0:T(8,128)(2,1)} %param.12) | copy-start | bytes 11010052
  4.6 5.3 %copy-start.5 = (bf16[256,1792]{1,0:T(8,128)(2,1)S(1)}, bf16[256,1792]{1,0:T(8,128)(2,1)}, u32[]{:S(2)}) copy-start(bf16[256,1792]{1,0:T(8,128)(2,1)} %param.15) | copy-start | bytes 2752516
  8.4 1.9 %copy-start.6 = (bf16[256,1792]{1,0:T(8,128)(2,1)S(1)}, bf16[256,1792]{1,0:T(8,128)(2,1)}, u32[]{:S(2)}) copy-start(bf16[256,1792]{1,0:T(8,128)(2,1)} %param.16) | copy-start | bytes 2752516
  8.4 4.1 %copy-start.8 = (f32[64,2]{0,1:T(2,128)S(1)}, f32[64,2]{0,1:T(2,128)}, u32[]{:S(2)}) copy-start(f32[64,2]{0,1:T(2,128)} %param.11) | copy-start | bytes 1540
  8.4 4.1 %copy-start.9 = (s32[64,2]{0,1:T(2,128)S(1)}, s32[64,2]{0,1:T(2,128)}, u32[]{:S(2)}) copy-start(s32[64,2]{0,1:T(2,128)} %param.10) | copy-start | bytes 1540
  12.5 13.6 %collective-permute-start = (bf16[32,2560]{1,0:T(8,128)(2,1)}, bf16[32,2560]{1,0:T(8,128)(2,1)}, u32[]{:S(2)}, u32[]{:S(2)}) collective-permute-start(bf16[32,2560]{1,0:T(8,128)(2,1)} %select_convert_fusion.2), channel_id=1, source_target_pairs={{0,1},{1,0},{2,3},{3,2},{4,5},{5,4},{6,7},{7,6},{8,9},{9,8},{10,11... | collective-permute-start | bytes 491528 | tf_op jit(solution)/shard_map/ppermute | solution.py:17
  26.0 7.4 %copy-start.4 = (bf16[1,1792,1024]{2,1,0:T(8,128)(2,1)S(1)}, bf16[1,1792,1024]{2,1,0:T(8,128)(2,1)}, u32[]{:S(2)}) copy-start(bf16[1,1792,1024]{2,1,0:T(8,128)(2,1)} %param.13) | copy-start | bytes 11010052
  27.2 15.3 %collective-permute-start.1 = (bf16[32,2560]{1,0:T(8,128)(2,1)S(1)}, bf16[32,2560]{1,0:T(8,128)(2,1)S(1)}, u32[]{:S(2)}, u32[]{:S(2)}) collective-permute-start(bf16[32,2560]{1,0:T(8,128)(2,1)S(1)} %fusion.46), channel_id=1, source_target_pairs={{0,2},{1,3},{2,0},{3,1},{4,6},{5,7},{6,4},{7,5},{8,10},{9,11},{10,... | collective-permute-start | bytes 491528 | tf_op jit(solution)/shard_map/ppermute | solution.py:17
  34.1 2.0 %copy-start.3 = (bf16[1,1792,1024]{2,1,0:T(8,128)(2,1)S(1)}, bf16[1,1792,1024]{2,1,0:T(8,128)(2,1)}, u32[]{:S(2)}) copy-start(bf16[1,1792,1024]{2,1,0:T(8,128)(2,1)} %param.12) | copy-start | bytes 11010052
  35.2 15.6 %collective-permute-start.5 = (bf16[64,2560]{1,0:T(8,128)(2,1)S(1)}, bf16[64,2560]{1,0:T(8,128)(2,1)S(1)}, u32[]{:S(2)}, u32[]{:S(2)}) collective-permute-start(bf16[64,2560]{1,0:T(8,128)(2,1)S(1)} %select_convert_fusion), channel_id=1, source_target_pairs={{0,1},{1,0},{2,3},{3,2},{4,5},{5,4},{6,7},{7,6},{8,9},{9,8},{10,11... | collective-permute-start | bytes 983048 | tf_op jit(solution)/shard_map/ppermute | solution.py:17
  42.4 9.7 %copy-start.1 = (bf16[1,1024,1792]{2,1,0:T(8,128)(2,1)S(1)}, bf16[1,1024,1792]{2,1,0:T(8,128)(2,1)}, u32[]{:S(2)}) copy-start(bf16[1,1024,1792]{2,1,0:T(8,128)(2,1)} %param.14) | copy-start | bytes 11010052
  42.4 1.9 %collective-permute-start.11 = (bf16[32,2560]{1,0:T(8,128)(2,1)S(1)}, bf16[32,2560]{1,0:T(8,128)(2,1)S(1)}, u32[]{:S(2)}, u32[]{:S(2)}) collective-permute-start(bf16[32,2560]{1,0:T(8,128)(2,1)S(1)} %select_convert_fusion.1), channel_id=1, source_target_pairs={{0,1},{1,0},{2,3},{3,2},{4,5},{5,4},{6,7},{7,6},{8,9},{9,8},{10,11... | collective-permute-start | bytes 491528 | tf_op jit(solution)/shard_map/ppermute | solution.py:17
  43.7 1.5 %collective-permute-start.2 = (bf16[32,1280]{1,0:T(8,128)(2,1)S(1)}, bf16[32,1280]{1,0:T(8,128)(2,1)S(1)}, u32[]{:S(2)}, u32[]{:S(2)}) collective-permute-start(bf16[32,1280]{1,0:T(8,128)(2,1)S(1)} %pad_maximum_fusion.4), channel_id=1, source_target_pairs={{0,1},{1,0},{2,3},{3,2},{4,5},{5,4},{6,7},{7,6},{8,9},{9,8},{10,11... | collective-permute-start | bytes 245768 | tf_op jit(solution)/shard_map/ppermute | solution.py:17
  44.3 6.2 %collective-permute-start.12 = (bf16[32,2560]{1,0:T(8,128)(2,1)S(1)}, bf16[32,2560]{1,0:T(8,128)(2,1)S(1)}, u32[]{:S(2)}, u32[]{:S(2)}) collective-permute-start(bf16[32,2560]{1,0:T(8,128)(2,1)S(1)} %fusion.47), channel_id=1, source_target_pairs={{0,2},{1,3},{2,0},{3,1},{4,6},{5,7},{6,4},{7,5},{8,10},{9,11},{10,... | collective-permute-start | bytes 491528 | tf_op jit(solution)/shard_map/ppermute | solution.py:17
  50.7 1.3 %collective-permute-start.13 = (bf16[32,1280]{1,0:T(8,128)(2,1)S(1)}, bf16[32,1280]{1,0:T(8,128)(2,1)S(1)}, u32[]{:S(2)}, u32[]{:S(2)}) collective-permute-start(bf16[32,1280]{1,0:T(8,128)(2,1)S(1)} %pad_maximum_fusion.5), channel_id=1, source_target_pairs={{0,1},{1,0},{2,3},{3,2},{4,5},{5,4},{6,7},{7,6},{8,9},{9,8},{10,11... | collective-permute-start | bytes 245768 | tf_op jit(solution)/shard_map/ppermute | solution.py:17
  50.9 10.2 %collective-permute-start.6 = (bf16[64,2560]{1,0:T(8,128)(2,1)S(1)}, bf16[64,2560]{1,0:T(8,128)(2,1)S(1)}, u32[]{:S(2)}, u32[]{:S(2)}) collective-permute-start(bf16[64,2560]{1,0:T(8,128)(2,1)S(1)} %fusion.45), channel_id=1, source_target_pairs={{0,2},{1,3},{2,0},{3,1},{4,6},{5,7},{6,4},{7,5},{8,10},{9,11},{10,... | collective-permute-start | bytes 983048 | tf_op jit(solution)/shard_map/ppermute | solution.py:17
  61.4 3.5 %collective-permute-start.7 = (bf16[64,1280]{1,0:T(8,128)(2,1)S(1)}, bf16[64,1280]{1,0:T(8,128)(2,1)S(1)}, u32[]{:S(2)}, u32[]{:S(2)}) collective-permute-start(bf16[64,1280]{1,0:T(8,128)(2,1)S(1)} %pad_maximum_fusion.3), channel_id=1, source_target_pairs={{0,1},{1,0},{2,3},{3,2},{4,5},{5,4},{6,7},{7,6},{8,9},{9,8},{10,11... | collective-permute-start | bytes 491528 | tf_op jit(solution)/shard_map/ppermute | solution.py:17
  61.7 19.0 %collective-permute-start.14 = (bf16[64,1792]{1,0:T(8,128)(2,1)S(1)}, bf16[64,1792]{1,0:T(8,128)(2,1)S(1)}, u32[]{:S(2)}, u32[]{:S(2)}) collective-permute-start(bf16[64,1792]{1,0:T(8,128)(2,1)S(1)} %fusion.32), channel_id=1, source_target_pairs={{0,8},{4,12},{8,0},{12,4},{1,9},{5,13},{9,1},{13,5},{2,10},{6,14},... | collective-permute-start | bytes 688136 | tf_op jit(solution)/shard_map/ppermute | solution.py:12
  65.9 20.0 %collective-permute-start.8 = (bf16[64,1792]{1,0:T(8,128)(2,1)S(1)}, bf16[64,1792]{1,0:T(8,128)(2,1)S(1)}, u32[]{:S(2)}, u32[]{:S(2)}) collective-permute-start(bf16[64,1792]{1,0:T(8,128)(2,1)S(1)} %get-tuple-element.5), channel_id=1, source_target_pairs={{0,12},{4,0},{8,4},{12,8},{1,13},{5,1},{9,5},{13,9},{2,14},{6,2},{... | collective-permute-start | bytes 688136 | tf_op jit(solution)/shard_map/ppermute | solution.py:12
  68.3 17.6 %collective-permute-start.9 = (bf16[64,1792]{1,0:T(8,128)(2,1)S(1)}, bf16[64,1792]{1,0:T(8,128)(2,1)S(1)}, u32[]{:S(2)}, u32[]{:S(2)}) collective-permute-start(bf16[64,1792]{1,0:T(8,128)(2,1)S(1)} %get-tuple-element.6), channel_id=1, source_target_pairs={{0,4},{4,8},{8,12},{12,0},{1,5},{5,9},{9,13},{13,1},{2,6},{6,10},{... | collective-permute-start | bytes 688136 | tf_op jit(solution)/shard_map/ppermute | solution.py:12
